TPU v7x, 32 devices: a whole 2x2x4 slice. The times are simulated.
32 devices in a mesh: dp: 8 (over y, x, core), tensor: 4 (over z).
Axes of the slice: x: 2, y: 2, z: 4, core: 2. Of those that a mesh axis runs over, the one named last changes fastest.
Arguments:
- tokens: bfloat16 [4096, 2304], P(('dp', 'tensor')), may hold values from -6 to 6
- cotangent: bfloat16 [4096, 4096], P('dp', 'tensor'), may hold values from -6 to 6
- pre_gain: float32 [2304], replicated, may hold values from 0.25 to 1.75
- w_query: bfloat16 [2304, 4096], P('dp', 'tensor'), may hold values from -0.375 to 0.375
- key_weight: bfloat16 [2304, 2048], P('dp', 'tensor'), may hold values from -0.375 to 0.375
- value_weight: bfloat16 [2304, 2048], P('dp', 'tensor'), may hold values from -0.125 to 0.125
Outputs:
- attended: bfloat16 [4096, 4096], P('dp', 'tensor')
- grad_tokens: bfloat16 [4096, 2304], P(('dp', 'tensor'))
- grad_query: float32 [2304, 4096], P('dp', 'tensor')
- grad_key: float32 [2304, 2048], P('dp', 'tensor')
- grad_value: float32 [2304, 2048], P('dp', 'tensor')
- grad_pre_gain: float32 [2304], replicated
All inputs are finite; a program needn't handle non-finite values.
Results may differ from a plain program's by a relative error of at most 0.019.
The roundings to bfloat16 on the way count: a program that leaves them out, or rounds other values in their place, can miss the bound.
Values may be sent and summed in bfloat16 or wider, within the bound.
A program may use at most 192 MiB of HBM per device.

v0:
```python
import jax
import jax.numpy as jnp
from jax import lax
from jax.sharding import PartitionSpec as P

HEAD_SIZE = 128
SEQ_LEN = 64


EPS = 1e-06
CAP = 50.0
BASE = 10000.0
query_scalar = 144.0


def rotary_tables(segment_length, half):
    places = jnp.arange(segment_length, dtype=jnp.float32)[:, None]
    freqs = BASE ** (-jnp.arange(half, dtype=jnp.float32) / half)
    angles = places * freqs[None, :]
    return (jnp.cos(angles)[:, None, :], jnp.sin(angles)[:, None, :])


def rotate(values, cosine_table, sine_table):
    half = values.shape[-1] // 2
    first, second = (values[..., :half], values[..., half:])
    return jnp.concatenate(
        [first * cosine_table - second * sine_table, second * cosine_table + first * sine_table], -1
    )


def inverse_rotation(values, cosine_table, sine_table):
    half = values.shape[-1] // 2
    first, second = (values[..., :half], values[..., half:])
    return jnp.concatenate(
        [first * cosine_table + second * sine_table, second * cosine_table - first * sine_table], -1
    )


def attend_forward(query, key, value):
    repeat = query.shape[1] // key.shape[1]
    keys = jnp.repeat(key, repeat, axis=1)
    values = jnp.repeat(value, repeat, axis=1)
    factor = query_scalar ** (-0.5)
    raw = jnp.einsum("qhd,khd->hqk", query, keys, preferred_element_type=jnp.float32) * factor
    bent = jnp.tanh(raw / CAP)
    capped = CAP * bent
    segment_length = query.shape[0]
    causal = jnp.arange(segment_length)[None, :] <= jnp.arange(segment_length)[:, None]
    raised = jnp.where(causal[None], jnp.exp(capped), 0.0)
    weights = raised / jnp.sum(raised, -1, keepdims=True)
    probs = weights.astype(jnp.bfloat16)
    attended = jnp.einsum("hqk,khd->qhd", probs, values, preferred_element_type=jnp.float32).astype(
        jnp.bfloat16
    )
    return (attended, weights, probs, bent)


def attend_backward(d_attended, query, key, value, weights, probs, bent):
    repeat = query.shape[1] // key.shape[1]
    keys = jnp.repeat(key, repeat, axis=1)
    values = jnp.repeat(value, repeat, axis=1)
    factor = query_scalar ** (-0.5)
    d_probs = jnp.einsum("qhd,khd->hqk", d_attended, values, preferred_element_type=jnp.float32)
    d_capped = weights * (d_probs - jnp.sum(weights * d_probs, -1, keepdims=True))
    d_scores = (d_capped * (1.0 - bent * bent) * factor).astype(jnp.bfloat16)
    query_back = jnp.einsum("hqk,khd->qhd", d_scores, keys, preferred_element_type=jnp.float32)
    key_heads = jnp.einsum("hqk,qhd->khd", d_scores, query, preferred_element_type=jnp.float32)
    value_heads = jnp.einsum("hqk,qhd->khd", probs, d_attended, preferred_element_type=jnp.float32)
    segment_length, heads, width = query.shape
    key_rotated_back = key_heads.reshape(segment_length, heads // repeat, repeat, width).sum(2)
    value_returned = value_heads.reshape(segment_length, heads // repeat, repeat, width).sum(2)
    return (query_back, key_rotated_back, value_returned)


def segment_pass(query, key, value, d_attended):
    attended, weights, probs, bent = attend_forward(query, key, value)
    query_back, key_rotated_back, value_returned = attend_backward(
        d_attended, query, key, value, weights, probs, bent
    )
    return (attended, query_back, key_rotated_back, value_returned)


def per_device(tokens, cotangent, pre_gain, w_query, key_weight, value_weight):
    contract_first = (((0,), (0,)), ((), ()))
    contract_last = (((1,), (1,)), ((), ()))
    rows_f = tokens.astype(jnp.float32)
    inv_one = lax.rsqrt(jnp.mean(rows_f * rows_f, -1, keepdims=True) + EPS)
    unit_one = rows_f * inv_one
    normed_input = (unit_one * pre_gain).astype(jnp.bfloat16)
    gathered = lax.all_gather(normed_input, "tensor", axis=0, tiled=True)
    segment_length = gathered.shape[0]
    token_span = SEQ_LEN
    pieces_count = segment_length // token_span
    heads_query = w_query.shape[1] // HEAD_SIZE
    heads_key = key_weight.shape[1] // HEAD_SIZE
    pieces = (
        lax.all_gather(w_query, "dp", axis=0, tiled=True),
        lax.all_gather(key_weight, "dp", axis=0, tiled=True),
        lax.all_gather(value_weight, "dp", axis=0, tiled=True),
    )
    query_raw, key_unrotated, value_projected = tuple(
        (jnp.dot(gathered, piece, preferred_element_type=jnp.float32) for piece in pieces)
    )
    cosine_table, sine_table = rotary_tables(token_span, HEAD_SIZE // 2)
    query = rotate(
        query_raw.reshape(pieces_count, token_span, heads_query, HEAD_SIZE),
        cosine_table,
        sine_table,
    ).astype(jnp.bfloat16)
    key = rotate(
        key_unrotated.reshape(pieces_count, token_span, heads_key, HEAD_SIZE),
        cosine_table,
        sine_table,
    ).astype(jnp.bfloat16)
    value = value_projected.reshape(pieces_count, token_span, heads_key, HEAD_SIZE).astype(
        jnp.bfloat16
    )
    d_attended = cotangent.reshape(pieces_count, token_span, heads_query, HEAD_SIZE)
    attended, query_back, key_rotated_back, value_returned = jax.vmap(segment_pass)(
        query, key, value, d_attended
    )
    attended_flat = attended.reshape(segment_length, heads_query * HEAD_SIZE)
    d_query = (
        inverse_rotation(query_back, cosine_table, sine_table)
        .astype(jnp.bfloat16)
        .reshape(segment_length, heads_query * HEAD_SIZE)
    )
    key_gradient = (
        inverse_rotation(key_rotated_back, cosine_table, sine_table)
        .astype(jnp.bfloat16)
        .reshape(segment_length, heads_key * HEAD_SIZE)
    )
    value_gradient = value_returned.astype(jnp.bfloat16).reshape(
        segment_length, heads_key * HEAD_SIZE
    )
    back_query, back_key, back_value = (
        lax.all_gather(w_query, "dp", axis=0, tiled=True),
        lax.all_gather(key_weight, "dp", axis=0, tiled=True),
        lax.all_gather(value_weight, "dp", axis=0, tiled=True),
    )
    joined = jnp.concatenate([d_query, key_gradient, value_gradient], 1)
    block = gathered
    grads = lax.psum_scatter(
        lax.dot_general(block, joined, contract_first, preferred_element_type=jnp.float32).astype(
            jnp.bfloat16
        ),
        "dp",
        scatter_dimension=0,
        tiled=True,
    ).astype(jnp.float32)
    width_query = w_query.shape[1]
    width_key = key_weight.shape[1]
    grad_query = grads[:, :width_query]
    grad_key = grads[:, width_query : width_query + width_key]
    grad_value = grads[:, width_query + width_key :]
    total = jnp.zeros((tokens.shape[0] * lax.axis_size("tensor"), gathered.shape[1]), jnp.float32)
    for grad_part, weight in (
        (d_query, back_query),
        (key_gradient, back_key),
        (value_gradient, back_value),
    ):
        block = grad_part
        total = total + lax.dot_general(
            block, weight, contract_last, preferred_element_type=jnp.float32
        )
    d_normed = lax.psum_scatter(
        total.astype(jnp.bfloat16), "tensor", scatter_dimension=0, tiled=True
    ).astype(jnp.float32)
    pre_part = jnp.sum(d_normed * unit_one, 0)
    scaled_in = d_normed * pre_gain
    grad_tokens = (
        inv_one * (scaled_in - unit_one * jnp.mean(scaled_in * unit_one, -1, keepdims=True))
    ).astype(jnp.bfloat16)
    grad_pre = lax.psum(pre_part, ("dp", "tensor"))
    return (attended_flat, grad_tokens, grad_query, grad_key, grad_value, grad_pre)


def solution(mesh):
    placed = (
        P(("dp", "tensor"), None),
        P("dp", "tensor"),
        P(),
        P("dp", "tensor"),
        P("dp", "tensor"),
        P("dp", "tensor"),
    )
    return jax.shard_map(
        per_device,
        mesh=mesh,
        in_specs=placed,
        out_specs=(
            P("dp", "tensor"),
            P(("dp", "tensor"), None),
            P("dp", "tensor"),
            P("dp", "tensor"),
            P("dp", "tensor"),
            P(),
        ),
        check_vma=False,
    )
```

profile of v0, /device:TPU:0, one launch (start us, length us, event | category | flops | bytes accessed | tf_op | source)
XLA Modules:
  0.0 347.0 jit_solution(11530087274163512373)
XLA Ops:
  7.2 1.3 fusion.22
  8.6 2.1 fusion.20
  10.7 0.0 all-gather.7.cloned.1.call-start
  10.7 0.7 all-gather.7.cloned.1.call-update
  11.5 0.7 all-gather.11.cloned.1.call-update
  12.2 0.5 all-gather.9.cloned.1.call-update
  12.8 0.0 reduce-scatter.3.cloned.1.call-start
  12.8 0.3 copy.62
  13.1 0.1 fusion.34
  13.3 50.3 %all-gather.5.cloned.1.call-done = bf16[512,2304]{1,0:T(8,128)(2,1)} async-done(((bf16[128,2304]{1,0:T(8,128)(2,1)}), bf16[512,2304]{1,0:T(8,128)(2,1)}) %all-gather.5.cloned.1.call-update) | async-done | bytes 2359312 | tf_op jit(solution)/shard_map/all_gather | solution.py:90
  63.6 29.6 %all-gather.7.cloned.1.call-done = bf16[2304,512]{1,0:T(8,128)(2,1)} async-done(((bf16[288,512]{1,0:T(8,128)(2,1)}), bf16[2304,512]{1,0:T(8,128)(2,1)}) %all-gather.7.cloned.1.call-update) | async-done | bytes 2359312 | tf_op jit(solution)/shard_map/all_gather | solution.py:99
  93.1 3.8 %convolution_convert_fusion.2 = bf16[512,512]{1,0:T(8,128)(2,1)S(1)} fusion(bf16[512,2304]{1,0:T(8,128)(2,1)} %all-gather.5.cloned.1.call-done, bf16[2304,512]{1,0:T(8,128)(2,1)} %all-gather.7.cloned.1.call-done), kind=kOutput, calls=%fused_computation.36 | convolution fusion | flops 1208221696 | bytes 5242880 | tf_op jit(solution)/shard_map/dot_general | solution.py:102
  96.9 0.1 convert_element_type.61
  97.0 0.1 copy.41
  97.1 26.8 %all-gather.11.cloned.1.call-done = bf16[2304,512]{1,0:T(8,128)(2,1)} async-done(((bf16[288,512]{1,0:T(8,128)(2,1)}), bf16[2304,512]{1,0:T(8,128)(2,1)}) %all-gather.11.cloned.1.call-update) | async-done | bytes 2359312 | tf_op jit(solution)/shard_map/all_gather | solution.py:98
  123.9 4.7 %fusion.56 = f32[512,512]{1,0:T(8,128)} fusion(bf16[512,2304]{1,0:T(8,128)(2,1)} %all-gather.5.cloned.1.call-done, bf16[2304,512]{1,0:T(8,128)(2,1)} %all-gather.11.cloned.1.call-done), kind=kOutput, calls=%fused_computation.86 | convolution fusion | flops 1207959552 | bytes 5767168 | tf_op jit(solution)/shard_map/dot_general | solution.py:102
  128.6 1.6 reshape.112
  130.2 0.6 fusion.55
  130.8 0.3 subtract_convert_fusion.3
  131.2 0.3 pad_maximum_fusion.2
  131.5 0.2 broadcast_in_dim.12
  131.7 1.0 copy-done.4
  132.7 2.0 fusion.28
  134.7 29.7 %all-gather.9.cloned.1.call-done = bf16[2304,1024]{1,0:T(8,128)(2,1)} async-done(((bf16[288,1024]{1,0:T(8,128)(2,1)}), bf16[2304,1024]{1,0:T(8,128)(2,1)}) %all-gather.9.cloned.1.call-update) | async-done | bytes 4718608 | tf_op jit(solution)/shard_map/all_gather | solution.py:97
  164.5 5.3 %convolution_bitcast_fusion = f32[64,8,8,128]{3,1,2,0:T(8,128)S(1)} fusion(bf16[512,2304]{1,0:T(8,128)(2,1)} %all-gather.5.cloned.1.call-done, bf16[2304,1024]{1,0:T(8,128)(2,1)} %all-gather.9.cloned.1.call-done), kind=kOutput, calls=%fused_computation.22 | convolution fusion | flops 2415919104 | bytes 9175040 | tf_op jit(solution)/shard_map/dot_general | solution.py:102
  169.8 0.5 copy.60
  170.3 0.7 fusion.53
  171.0 0.9 subtract_convert_fusion.1
  171.9 0.2 broadcast_in_dim.18
  172.1 2.7 fusion.12
  174.9 7.5 %fusion.25 = f32[8,8,128,64]{2,3,1,0:T(8,128)} fusion(f32[8,8,64,64]{3,2,1,0:T(8,128)} %fusion.28, f32[8,8,64,64]{2,3,1,0:T(8,128)} %get-tuple-element.25, bf16[8,64,8,64]{3,1,2,0:T(8,128)(2,1)} %copy-done.8, bf16[8,64,8,64]{3,1,2,0:T(8,128)(2,1)S(1)} %get-tuple-element.8, f32[8,8,64]{2,1,0:T(8,128)S(1)} %get-tuple-element.24, ...), kind=kOutput, calls=%fused_computation.52 | convolution fusion | flops 73404480 | bytes 5263360 | tf_op jit(solution)/shard_map/vmap(hqk,qhd->khd)/dot_general | solution.py:67
  182.4 5.8 %convolution_bitcast_fusion.1 = f32[8,64,8,128]{3,1,2,0:T(8,128)S(1)} fusion(bf16[8,64,8,128]{3,1,2,0:T(8,128)(2,1)} %bitcast.91, f32[8,8,64,64]{3,2,1,0:T(8,128)} %fusion.28, f32[8,8,64,64]{2,3,1,0:T(8,128)} %get-tuple-element.25, f32[8,8,64]{2,1,0:T(8,128)S(1)} %get-tuple-element.24, pred[64,64]{0,1:T(8,128)(4,1)S(1)} %iota_compare_fusion), kind=kOutput, calls=%fused_computation.23 | convolution fusion | flops 71307328 | bytes 5263360 | tf_op jit(solution)/shard_map/vmap(hqk,khd->qhd)/dot_general | solution.py:66
  188.2 3.7 %fusion.26 = f32[8,8,64,128]{3,2,1,0:T(8,128)} fusion(bf16[8,64,8,128]{3,2,1,0:T(8,128)(2,1)S(1)} %bitcast.87, f32[8,8,64,64]{2,3,1,0:T(8,128)} %get-tuple-element.25, f32[8,8,64]{2,1,0:T(8,128)S(1)} %get-tuple-element.24, pred[64,64]{0,1:T(8,128)(4,1)S(1)} %iota_compare_fusion), kind=kOutput, calls=%fused_computation.53 | convolution fusion | flops 68419584 | bytes 4214784 | tf_op jit(solution)/shard_map/vmap(hqk,qhd->khd)/dot_general | solution.py:68
  191.9 1.9 reduce_sum.66
  193.8 2.7 reduce_sum.67
  196.5 1.5 copy.53
  197.9 0.4 add_convert_fusion.2
  198.4 0.8 add_convert_fusion
  199.2 0.6 pad_maximum_fusion.1
  199.8 0.9 copy.50
  200.7 0.3 pad_maximum_fusion.3
  201.0 0.4 copy.51
  201.5 2.7 fusion.46
  204.2 1.4 convolution_add_fusion.1
  205.6 0.2 copy-done.6
  205.8 2.9 fusion.1
  208.7 0.0 reduce-scatter.5.cloned.1.call-start
  208.8 0.3 copy.85
  209.0 0.7 copy-done.3
  209.7 0.1 copy_bitcast_fusion.2
  209.9 0.7 copy-done.12
  210.5 7.8 %convolution_convert_fusion = bf16[2304,2048]{1,0:T(8,128)(2,1)} fusion(bf16[512,2304]{1,0:T(8,128)(2,1)S(1)} %copy-done.12, bf16[512,512]{1,0:T(8,128)(2,1)S(1)} %get-tuple-element.26, bf16[512,512]{1,0:T(8,128)(2,1)S(1)} %get-tuple-element.27, bf16[512,1024]{1,0:T(8,128)(2,1)S(1)} %bitcast.94), kind=kOutput, calls=%fused_computation.1 | convolution fusion | flops 4842848256 | bytes 13893632 | tf_op jit(solution)/shard_map/dot_general | solution.py:144
  218.4 1.2 copy-done.5
  219.6 0.7 copy-done.13
  220.3 0.9 fusion.17
  221.1 0.7 copy.47
  221.8 1.2 copy.86
  223.1 33.5 %reduce-scatter.3.cloned.1.call-done = bf16[128,2304]{1,0:T(8,128)(2,1)} async-done(((bf16[512,2304]{1,0:T(8,128)(2,1)}), bf16[128,2304]{1,0:T(8,128)(2,1)}) %reduce-scatter.3.cloned.1.call-update) | async-done | bytes 589840 | tf_op jit(solution)/shard_map/reduce_scatter | solution.py:166
  256.6 1.5 fusion.23
  258.1 40.3 %psum.7 = f32[2304]{0:T(1024)} all-reduce(f32[2304]{0:T(1024)S(1)} %get-tuple-element.6), channel_id=1, replica_groups=mesh['dp'=8,'tensor'=4] {'dp','tensor'}, use_global_device_ids=true, to_apply=%region_9.10 | all-reduce | flops 2304 | bytes 18432 | tf_op jit(solution)/shard_map/psum | solution.py:174
  298.4 2.3 fusion.19
  300.7 36.1 %reduce-scatter.5.cloned.1.call-done = bf16[288,2048]{1,0:T(8,128)(2,1)} async-done(((bf16[2304,2048]{1,0:T(8,128)(2,1)}), bf16[288,2048]{1,0:T(8,128)(2,1)}) %reduce-scatter.5.cloned.1.call-update) | async-done | bytes 1179664 | tf_op jit(solution)/shard_map/reduce_scatter | solution.py:143
  336.7 2.3 slice.52
  339.0 1.2 fusion.54
  (37 shorter events, 0.3 us)
Async XLA Ops:
  7.2 5.6 %copy-start.10 = (bf16[512,1024]{1,0:T(8,128)(2,1)S(1)}, bf16[512,1024]{1,0:T(8,128)(2,1)}, u32[]{:S(2)}) copy-start(bf16[512,1024]{1,0:T(8,128)(2,1)} %param.7) | copy-start | bytes 3145732
  7.2 56.4 %all-gather.5.cloned.1.call-start = ((), (), s32[]{:S(2)}) async-start(), calls=%async_computation.2 | async-start | bytes 2949120 | tf_op jit(solution)/shard_map/all_gather | solution.py:90
  10.7 82.4 %all-gather.7.cloned.1.call-start = ((), (), s32[]{:S(2)}) async-start(), calls=%async_computation.3 | async-start | bytes 2654208 | tf_op jit(solution)/shard_map/all_gather | solution.py:99
  11.4 112.5 %all-gather.11.cloned.1.call-start = ((), (), s32[]{:S(2)}) async-start(), calls=%async_computation.5 | async-start | bytes 2654208 | tf_op jit(solution)/shard_map/all_gather | solution.py:98
  12.2 152.3 %all-gather.9.cloned.1.call-start = ((), (), s32[]{:S(2)}) async-start(), calls=%async_computation.4 | async-start | bytes 5308416 | tf_op jit(solution)/shard_map/all_gather | solution.py:97
  12.8 243.8 %reduce-scatter.3.cloned.1.call-start = ((), (), s32[]{:S(2)}) async-start(), calls=%async_computation.6 | async-start | bytes 2949120 | tf_op jit(solution)/shard_map/reduce_scatter | solution.py:166
  131.7 1.0 copy-start.4
  171.9 3.0 copy-start.8
  172.1 2.8 copy-start.9
  197.9 7.7 %copy-start.2 = (bf16[8,64,4,128]{3,2,1,0:T(4,128)(2,1)}, bf16[8,64,4,128]{3,2,1,0:T(4,128)(2,1)S(1)}, u32[]{:S(2)}) copy-start(bf16[8,64,4,128]{3,2,1,0:T(4,128)(2,1)S(1)} %copy.53) | copy-start | bytes 1572868
  198.4 3.1 slice-start
  199.2 2.3 slice-start.1
  201.5 2.7 copy-start.7
  204.2 1.7 copy-start.6
  208.7 1.0 copy-start.3
  208.7 128.0 %reduce-scatter.5.cloned.1.call-start = ((), (), s32[]{:S(2)}) async-start(), calls=%async_computation.7 | async-start | bytes 10616832 | tf_op jit(solution)/shard_map/reduce_scatter | solution.py:143
  208.7 1.8 copy-start.12
  218.3 1.2 copy-start.5
  218.3 1.9 copy-start.13
  221.1 35.5 %copy-start = (bf16[128,2304]{1,0:T(8,128)(2,1)S(1)}, bf16[128,2304]{1,0:T(8,128)(2,1)}, u32[]{:S(2)}) copy-start(bf16[128,2304]{1,0:T(8,128)(2,1)} %param.6) | copy-start | bytes 1769476
  221.1 35.4 %copy-start.11 = (f32[2304]{0:T(1024)S(1)}, f32[2304]{0:T(1024)}, u32[]{:S(2)}) copy-start(f32[2304]{0:T(1024)} %param.8) | copy-start | bytes 27652
  336.7 2.3 copy-start.1
Sparse Core Ops, SparseCore 0:
  10.8 52.6 all-gather.4
  65.4 27.6 all-gather.6
  95.0 28.8 all-gather.10
  125.7 38.7 all-gather.8
  208.8 47.6 reduce-scatter.2
  259.9 76.7 reduce-scatter.4
where the time goes:
time: 348 us; the launch traced here: 347 us
  waiting for transfers between devices  208 us (60%)
  matrix products  51.2 us (15%)
  blocking collectives  40.3 us (12%)
  local copies, waits for them, and re-layouts  17.4 us (5%)
  other arithmetic  15.6 us (4%)
  between operations  14.5 us (4%)
    all_gather x1, waiting for transfers between devices, per_device(): gathered = lax.all_gather(normed_input, 'tensor', axis=0, tiled=True)  50.3 us
    psum x1, blocking collectives, per_device(): grad_pre = lax.psum(pre_part, ('dp', 'tensor'))  40.3 us
    reduce_scatter x1, waiting for transfers between devices, per_device(): lax.psum_scatter(lax.dot_general(block, joined, contract_first, preferred...  36.1 us
    reduce_scatter x1, waiting for transfers between devices, per_device(): lax.psum_scatter(total.astype(jnp.bfloat16), 'tensor', scatter_dimension=...  33.5 us
    all_gather x1, waiting for transfers between devices, per_device(): lax.all_gather(w_query, 'dp', axis=0, tiled=True)  29.7 us
    all_gather x1, waiting for transfers between devices, per_device(): lax.all_gather(value_weight, 'dp', axis=0, tiled=True)  29.6 us
    all_gather x1, waiting for transfers between devices, per_device(): lax.all_gather(key_weight, 'dp', axis=0, tiled=True)  26.8 us
    dot_general x3, matrix products, per_device(): jnp.dot(gathered, piece, preferred_element_type=jnp.float32)  13.8 us
  transfers between devices with their start and end apart: 6, of which 6 were waited for; matrix products, arithmetic and copies ran while one was open for 8% of the time, Pallas kernels for 0%

commit v1 on v0

--- a/solution.py
+++ b/solution.py
@@ -1,6 +1,10 @@
+import functools
+
 import jax
 import jax.numpy as jnp
 from jax import lax
+from jax.experimental import pallas as pl
+from jax.experimental.pallas import tpu as pltpu
 from jax.sharding import PartitionSpec as P
 
 HEAD_SIZE = 128
@@ -175,7 +179,537 @@
     return (attended_flat, grad_tokens, grad_query, grad_key, grad_value, grad_pre)
 
 
+F32 = jnp.float32
+BF16 = jnp.bfloat16
+NN = (((1,), (0,)), ((), ()))
+NT = (((1,), (1,)), ((), ()))
+TN = (((0,), (0,)), ((), ()))
+
+
+def swap_halves(values):
+    half = values.shape[-1] // 2
+    return jnp.concatenate([values[:, half:], values[:, :half]], -1)
+
+
+def whole_kernel(
+    dims,
+    tok_ref,
+    gain_ref,
+    own_ref,
+    cot_ref,
+    cos_ref,
+    sin_ref,
+    mask_ref,
+    att_ref,
+    gtok_ref,
+    grad_ref,
+    gpre_ref,
+    x,
+    xt,
+    w,
+    proj,
+    dproj,
+    g,
+    pr,
+    cs,
+    dr,
+    ar,
+    dn,
+    rb,
+    pb1,
+    pb2,
+    ws,
+    wr,
+    xs,
+    xr,
+    gs,
+    gr,
+    zs,
+    zr,
+    ps,
+    prs,
+):
+    n_dp, n_t, chunks, rep, hd = dims
+    dp = lax.axis_index("dp")
+    t = lax.axis_index("tensor")
+    rows = tok_ref.shape[0]
+    width = tok_ref.shape[1]
+    shard = own_ref.shape[1]
+    half = shard // 2
+    core = lax.rem(dp, 2)
+    chip = lax.div(dp, 2)
+    mate, px, py = dp ^ 1, dp ^ 2, dp ^ 4
+
+    barrier = pltpu.get_barrier_semaphore()
+    for o in range(1, n_dp):
+        pl.semaphore_signal(
+            barrier, inc=1, device_id=(dp ^ o, t), device_id_type=pl.DeviceIdType.MESH
+        )
+    for o in range(1, n_t):
+        pl.semaphore_signal(
+            barrier, inc=1, device_id=(dp, t ^ o), device_id_type=pl.DeviceIdType.MESH
+        )
+    pl.semaphore_wait(barrier, n_dp + n_t - 2)
+
+    def rdma(src, dst, ssem, rsem, d, z):
+        return pltpu.make_async_remote_copy(
+            src_ref=src,
+            dst_ref=dst,
+            send_sem=ssem,
+            recv_sem=rsem,
+            device_id=(d, z),
+            device_id_type=pl.DeviceIdType.MESH,
+        )
+
+    def wrow(who, h=None):
+        if h is None:
+            return pl.ds(pl.multiple_of(who * shard, 16), shard)
+        return pl.ds(pl.multiple_of(who * shard + h * half, 16), half)
+
+    def wcopy(kind, j, origin, to, src=None, h=None):
+        place = w.at[j, wrow(origin, h)]
+        return rdma(place if src is None else src, place, ws.at[kind, j], wr.at[kind, j], to, t)
+
+    for j in range(chunks):
+        wcopy(0, j, dp, px, own_ref.at[j]).start()
+        wcopy(1, j, dp, py, own_ref.at[j]).start()
+
+    tokens = tok_ref[...].astype(F32)
+    inv = lax.rsqrt(jnp.mean(tokens * tokens, -1, keepdims=True) + EPS)
+    x[pl.ds(pl.multiple_of(t * rows, rows), rows), :] = (
+        (tokens * inv) * gain_ref[...]
+    ).astype(BF16)
+
+    def xcopy(way, o, origin, to):
+        place = x.at[pl.ds(pl.multiple_of(origin * rows, rows), rows)]
+        return rdma(place, place, xs.at[way, o], xr.at[way, o], dp, to)
+
+    @pl.when(t < n_t - 1)
+    def _():
+        xcopy(0, 0, t, t + 1).start()
+
+    @pl.when(t > 0)
+    def _():
+        xcopy(1, 0, t, t - 1).start()
+
+    for j in range(chunks):
+        wcopy(2, j, dp, mate, own_ref.at[j]).start()
+        w[j, wrow(dp), :] = own_ref[j]
+
+    def relay(j):
+        wcopy(0, j, px, px).wait_recv()
+        wcopy(5, j, px, py, h=0).start()
+        wcopy(3, j, px, mate).start()
+        wcopy(1, j, py, py).wait_recv()
+        wcopy(6, j, py, px, h=1).start()
+        wcopy(4, j, py, mate).start()
+
+    def xrelay(o):
+        @pl.when(t - o >= 0)
+        def _():
+            xcopy(0, o - 1, t - o, t).wait_recv()
+
+            @pl.when(t + 1 < n_t)
+            def _():
+                xcopy(0, o, t - o, t + 1).start()
+
+        @pl.when(t + o < n_t)
+        def _():
+            xcopy(1, o - 1, t + o, t).wait_recv()
+
+            @pl.when(t > 0)
+            def _():
+                xcopy(1, o, t + o, t - 1).start()
+
+    def far(j):
+        wcopy(5, j, dp ^ 6, py, h=0).wait_recv()
+        wcopy(6, j, dp ^ 6, px, h=1).wait_recv()
+        wcopy(7, j, dp ^ 6, mate).start()
+
+    relay(0)
+    relay(1)
+    xrelay(1)
+    relay(2)
+    relay(3)
+    xrelay(2)
+    for j in range(chunks):
+        far(j)
+    xrelay(3)
+    for j in range(chunks):
+        wcopy(2, j, mate, mate).wait_recv()
+        wcopy(3, j, dp ^ 3, mate).wait_recv()
+        wcopy(4, j, dp ^ 5, mate).wait_recv()
+        wcopy(7, j, dp ^ 7, mate).wait_recv()
+
+    qw = rep * hd
+    cw = qw + 2 * hd
+    factor = query_scalar ** (-0.5)
+    blocks = x.shape[0] // rows
+
+    xt[...] = x[...].T
+
+    def head(j, carry):
+        proj[...] = lax.dot_general(x[...], w[j], NN, preferred_element_type=F32)
+
+        def block(r, c2):
+            here = pl.ds(pl.multiple_of(r * rows, rows), rows)
+            cosv, sinv = cos_ref[...], sin_ref[...]
+
+            def turn(v):
+                return v * cosv + swap_halves(v) * sinv
+
+            def unturn(v):
+                return v * cosv - swap_halves(v) * sinv
+
+            q = jnp.concatenate(
+                [turn(proj[here, i * hd : (i + 1) * hd]).astype(BF16) for i in range(rep)], 0
+            )
+            k = turn(proj[here, qw : qw + hd]).astype(BF16)
+            v = proj[here, qw + hd : cw].astype(BF16)
+            cot = jnp.concatenate(
+                [cot_ref[j, here, i * hd : (i + 1) * hd] for i in range(rep)], 0
+            )
+            bent = jnp.tanh(
+                lax.dot_general(q, k, NT, preferred_element_type=F32) * factor / CAP
+            )
+            raised = jnp.exp(CAP * bent) * mask_ref[...]
+            weights = raised / jnp.sum(raised, -1, keepdims=True)
+            probs = weights.astype(BF16)
+            att = lax.dot_general(probs, v, NN, preferred_element_type=F32).astype(BF16)
+            d_probs = lax.dot_general(cot, v, NT, preferred_element_type=F32)
+            d_capped = weights * (d_probs - jnp.sum(weights * d_probs, -1, keepdims=True))
+            ds = (d_capped * (1.0 - bent * bent) * factor).astype(BF16)
+            dq = lax.dot_general(ds, k, NN, preferred_element_type=F32)
+            dk = lax.dot_general(ds, q, TN, preferred_element_type=F32)
+            dv = lax.dot_general(probs, cot, TN, preferred_element_type=F32)
+            for i in range(rep):
+                part = slice(i * rows, (i + 1) * rows)
+                att_ref[j, here, i * hd : (i + 1) * hd] = att[part]
+                dproj[j, here, i * hd : (i + 1) * hd] = unturn(dq[part]).astype(BF16)
+            dproj[j, here, qw : qw + hd] = unturn(dk).astype(BF16)
+            dproj[j, here, qw + hd : cw] = dv.astype(BF16)
+            return c2
+
+        lax.fori_loop(0, blocks, block, 0)
+        return carry
+
+    lax.fori_loop(0, chunks, head, 0)
+
+    low = t < n_t // 2
+    sign = jnp.where(low, 1, -1)
+    m = jnp.where(low, t, n_t - 1 - t)
+    fwd = jnp.where(low, 0, 1)
+
+    def mirror(b):
+        return jnp.where(low, b, n_t - 1 - b)
+
+    def zcopy(way, b, to):
+        src = dn.at[pl.ds(pl.multiple_of(b * rows, rows), rows)]
+        return rdma(src, rb.at[way, b], zs.at[way, b], zr.at[way, b], dp, to)
+
+    tile = 256
+
+    def back(i, carry):
+        b = mirror(n_t - 1 - i)
+        here = pl.ds(pl.multiple_of(b * rows, rows), rows)
+
+        def cols(n, c2):
+            span = pl.ds(pl.multiple_of(n * tile, tile), tile)
+            total = jnp.zeros((rows, tile), F32)
+            for j in range(chunks):
+                total += lax.dot_general(
+                    dproj[j, here, :], w[j, span, :], NT, preferred_element_type=F32
+                )
+            dn[here, span] = total.astype(BF16)
+            return c2
+
+        lax.fori_loop(0, width // tile, cols, 0)
+
+        @pl.when((m == 0) & (i < n_t - 1))
+        def _():
+            zcopy(fwd, b, t + sign).start()
+
+        return carry
+
+    lax.fori_loop(0, n_t, back, 0)
+
+    def gcopy(kind, j, src, dst, to):
+        return rdma(src, dst, gs.at[kind, j], gr.at[kind, j], to, t)
+
+    def to_mate(j):
+        return gcopy(0, j, g.at[j, :, 1 - core], pr.at[j], mate)
+
+    lo, hi = pl.ds(0, half), pl.ds(half, half)
+    cx, cy, cd = chip ^ 1, chip ^ 2, chip ^ 3
+
+    def d_x(j):
+        return gcopy(1, j, cs.at[j, cd, lo], dr.at[j, lo], px)
+
+    def d_y(j):
+        return gcopy(2, j, cs.at[j, cd, hi], dr.at[j, hi], py)
+
+    def x_lo(j):
+        return gcopy(3, j, cs.at[j, cx, lo], ar.at[0, j, lo], px)
+
+    def x_hi(j):
+        return gcopy(4, j, cs.at[j, cx, hi], ar.at[0, j, hi], px)
+
+    def y_lo(j):
+        return gcopy(5, j, cs.at[j, cy, lo], ar.at[1, j, lo], py)
+
+    def y_hi(j):
+        return gcopy(6, j, cs.at[j, cy, hi], ar.at[1, j, hi], py)
+
+    def add(*parts):
+        total = parts[0].astype(F32)
+        for part in parts[1:]:
+            total = total + part.astype(F32)
+        return total.astype(BF16)
+
+    def product(j):
+        for c in range(n_dp // 2):
+            for k in range(2):
+                who = 2 * c + k
+                g[j, c, k] = lax.dot_general(
+                    xt[who * shard : (who + 1) * shard, :],
+                    dproj[j],
+                    NN,
+                    preferred_element_type=F32,
+                ).astype(BF16)
+
+    def on_chip(j):
+        to_mate(j).wait_recv()
+        for c in range(n_dp // 2):
+            cs[j, c] = add(g[j, c, core], pr[j, c])
+        d_x(j).start()
+        d_y(j).start()
+        x_lo(j).start()
+        y_hi(j).start()
+
+    def pass_on(j):
+        d_x(j).wait_recv()
+        cs[j, cy, lo] = add(cs[j, cy, lo], dr[j, lo])
+        y_lo(j).start()
+        d_y(j).wait_recv()
+        cs[j, cx, hi] = add(cs[j, cx, hi], dr[j, hi])
+        x_hi(j).start()
+
+    def grads_step(j, carry):
+        @pl.when(j < chunks)
+        def _():
+            product(j)
+            to_mate(j).start()
+
+        @pl.when(j > 0)
+        def _():
+            on_chip(j - 1)
+
+        return carry
+
+    lax.fori_loop(0, chunks + 1, grads_step, 0)
+
+    def zsum(way, b):
+        here = pl.ds(pl.multiple_of(b * rows, rows), rows)
+        zcopy(way, b, t).wait_recv()
+        dn[here, :] = add(dn[here, :], rb[way, b])
+
+    @pl.when(m > 0)
+    def _():
+        b = mirror(n_t - 1)
+        zsum(fwd, b)
+        zcopy(fwd, b, t + sign).start()
+
+    pass_on(0)
+    pass_on(1)
+
+    @pl.when(m > 0)
+    def _():
+        b = mirror(0)
+        zsum(1 - fwd, b)
+        zcopy(1 - fwd, b, t - sign).start()
+        b2 = mirror(n_t - 2)
+        zsum(fwd, b2)
+        zcopy(fwd, b2, t + sign).start()
+
+    pass_on(2)
+    pass_on(3)
+
+    mine = pl.ds(pl.multiple_of(t * rows, rows), rows)
+    zcopy(1 - fwd, t, t).wait_recv()
+
+    @pl.when(m > 0)
+    def _():
+        zcopy(fwd, t, t).wait_recv()
+
+    @pl.when(m == 0)
+    def _():
+        rb[fwd, t] = jnp.zeros((rows, width), BF16)
+
+    d_normed = dn[mine, :].astype(F32) + rb[0, t].astype(F32) + rb[1, t].astype(F32)
+    tokens2 = tok_ref[...].astype(F32)
+    inv2 = lax.rsqrt(jnp.mean(tokens2 * tokens2, -1, keepdims=True) + EPS)
+    unit = tokens2 * inv2
+    pb1[dp] = jnp.sum(d_normed * unit, 0, keepdims=True)
+
+    def p1(o):
+        return rdma(pb1.at[dp], pb1.at[dp], ps.at[0, o], prs.at[0, o], dp ^ o, t)
+
+    def p2(o):
+        return rdma(pb2.at[t], pb2.at[t], ps.at[1, o], prs.at[1, o], dp, t ^ o)
+
+    def p1r(o):
+        return rdma(pb1.at[dp ^ o], pb1.at[dp ^ o], ps.at[0, o], prs.at[0, o], dp ^ o, t)
+
+    def p2r(o):
+        return rdma(pb2.at[t ^ o], pb2.at[t ^ o], ps.at[1, o], prs.at[1, o], dp, t ^ o)
+
+    for o in range(1, n_dp):
+        p1(o).start()
+    e = d_normed * gain_ref[...]
+    gtok_ref[...] = (inv2 * (e - unit * jnp.mean(e * unit, -1, keepdims=True))).astype(BF16)
+    for o in range(1, n_dp):
+        p1r(o).wait_recv()
+    total = pb1[0]
+    for o in range(1, n_dp):
+        total = total + pb1[o]
+    pb2[t] = total
+    for o in range(1, n_t):
+        p2(o).start()
+
+    for j in range(chunks):
+        x_lo(j).wait_recv()
+        y_hi(j).wait_recv()
+        y_lo(j).wait_recv()
+        x_hi(j).wait_recv()
+        grad_ref[j] = add(cs[j, chip], ar[0, j], ar[1, j])
+
+    for o in range(1, n_t):
+        p2r(o).wait_recv()
+    total = pb2[0]
+    for o in range(1, n_t):
+        total = total + pb2[o]
+    gpre_ref[...] = total
+
+    for j in range(chunks):
+        wcopy(0, j, dp, px, own_ref.at[j]).wait_send()
+        wcopy(1, j, dp, py, own_ref.at[j]).wait_send()
+        wcopy(2, j, dp, mate, own_ref.at[j]).wait_send()
+        wcopy(3, j, px, mate).wait_send()
+        wcopy(4, j, py, mate).wait_send()
+        wcopy(5, j, px, py, h=0).wait_send()
+        wcopy(6, j, py, px, h=1).wait_send()
+        wcopy(7, j, dp ^ 6, mate).wait_send()
+        to_mate(j).wait_send()
+        for copy in (d_x, d_y, x_lo, x_hi, y_lo, y_hi):
+            copy(j).wait_send()
+    for o in range(n_t - 1):
+        @pl.when((t - o >= 0) & (t + 1 < n_t))
+        def _():
+            xcopy(0, o, t - o, t + 1).wait_send()
+
+        @pl.when((t + o < n_t) & (t > 0))
+        def _():
+            xcopy(1, o, t + o, t - 1).wait_send()
+
+    for b in range(n_t - 1, 0, -1):
+        @pl.when(m < b)
+        def _():
+            zcopy(fwd, mirror(b), t + sign).wait_send()
+
+    @pl.when(m > 0)
+    def _():
+        zcopy(1 - fwd, mirror(0), t - sign).wait_send()
+
+    for o in range(1, n_dp):
+        p1(o).wait_send()
+    for o in range(1, n_t):
+        p2(o).wait_send()
+
+
+def fused_per_device(tokens, cotangent, pre_gain, w_query, key_weight, value_weight):
+    n_dp, n_t = lax.axis_size("dp"), lax.axis_size("tensor")
+    rows, width = tokens.shape
+    block = rows * n_t
+    shard = w_query.shape[0]
+    chunks = key_weight.shape[1] // HEAD_SIZE
+    rep = w_query.shape[1] // key_weight.shape[1]
+    qw = rep * HEAD_SIZE
+    cw = qw + 2 * HEAD_SIZE
+    parts = (
+        w_query.reshape(shard, chunks, qw),
+        key_weight.reshape(shard, chunks, HEAD_SIZE),
+        value_weight.reshape(shard, chunks, HEAD_SIZE),
+    )
+    own = jnp.concatenate(parts, -1).transpose(1, 0, 2)
+    cot = cotangent.reshape(block, chunks, qw).transpose(1, 0, 2)
+    cosine, sine = rotary_tables(SEQ_LEN, HEAD_SIZE // 2)
+    reps = rows // SEQ_LEN
+    cosine = jnp.tile(jnp.concatenate([cosine[:, 0], cosine[:, 0]], -1), (reps, 1))
+    sine = jnp.tile(jnp.concatenate([-sine[:, 0], sine[:, 0]], -1), (reps, 1))
+    place = jnp.arange(rows)
+    mask = (place[None, :] <= place[:, None]) & (
+        place[None, :] // SEQ_LEN == place[:, None] // SEQ_LEN
+    )
+    mask = jnp.tile(mask.astype(F32), (rep, 1))
+    vmem = pl.BlockSpec(memory_space=pltpu.VMEM)
+    dma = pltpu.SemaphoreType.DMA
+    att, grad_tokens, grads, grad_pre = pl.pallas_call(
+        functools.partial(whole_kernel, (n_dp, n_t, chunks, rep, HEAD_SIZE)),
+        out_shape=(
+            jax.ShapeDtypeStruct((chunks, block, qw), BF16),
+            jax.ShapeDtypeStruct((rows, width), BF16),
+            jax.ShapeDtypeStruct((chunks, shard, cw), BF16),
+            jax.ShapeDtypeStruct((1, width), F32),
+        ),
+        in_specs=[vmem] * 7,
+        out_specs=(vmem,) * 4,
+        scratch_shapes=[
+            pltpu.VMEM((block, width), BF16),
+            pltpu.VMEM((width, block), BF16),
+            pltpu.VMEM((chunks, width, cw), BF16),
+            pltpu.VMEM((block, cw), F32),
+            pltpu.VMEM((chunks, block, cw), BF16),
+            pltpu.VMEM((chunks, n_dp // 2, 2, shard, cw), BF16),
+            pltpu.VMEM((chunks, n_dp // 2, shard, cw), BF16),
+            pltpu.VMEM((chunks, n_dp // 2, shard, cw), BF16),
+            pltpu.VMEM((chunks, shard, cw), BF16),
+            pltpu.VMEM((2, chunks, shard, cw), BF16),
+            pltpu.VMEM((block, width), BF16),
+            pltpu.VMEM((2, n_t, rows, width), BF16),
+            pltpu.VMEM((n_dp, 1, width), F32),
+            pltpu.VMEM((n_t, 1, width), F32),
+            dma((8, chunks)),
+            dma((8, chunks)),
+            dma((2, n_t)),
+            dma((2, n_t)),
+            dma((7, chunks)),
+            dma((7, chunks)),
+            dma((2, n_t)),
+            dma((2, n_t)),
+            dma((2, n_dp)),
+            dma((2, n_dp)),
+        ],
+        compiler_params=pltpu.CompilerParams(
+            collective_id=0, has_side_effects=True, vmem_limit_bytes=62 * 1024 * 1024
+        ),
+    )(tokens, pre_gain[None, :], own, cot, cosine, sine, mask)
+    attended = att.transpose(1, 0, 2).reshape(block, chunks * qw)
+    grads = grads.astype(F32)
+    grad_query = grads[:, :, :qw].transpose(1, 0, 2).reshape(shard, chunks * qw)
+    grad_key = grads[:, :, qw : qw + HEAD_SIZE].transpose(1, 0, 2)
+    grad_value = grads[:, :, qw + HEAD_SIZE :].transpose(1, 0, 2)
+    return (
+        attended,
+        grad_tokens,
+        grad_query,
+        grad_key.reshape(shard, chunks * HEAD_SIZE),
+        grad_value.reshape(shard, chunks * HEAD_SIZE),
+        grad_pre[0],
+    )
+
+
 def solution(mesh):
+    fused = mesh.shape["dp"] == 8 and mesh.shape["tensor"] == 4
     placed = (
         P(("dp", "tensor"), None),
         P("dp", "tensor"),
@@ -185,7 +719,7 @@
         P("dp", "tensor"),
     )
     return jax.shard_map(
-        per_device,
+        fused_per_device if fused else per_device,
         mesh=mesh,
         in_specs=placed,
         out_specs=(

time: 348 us -> 155 us (0.45)
  waiting for transfers between devices: 208 us -> 0 us
  Pallas kernels: 0 us -> 138 us
  matrix products: 51.2 us -> 0 us
  blocking collectives: 40.3 us -> 0 us
  between operations: 14.5 us -> 0.78 us
  other arithmetic: 15.6 us -> 3.66 us
  local copies, waits for them, and re-layouts: 17.4 us -> 12.2 us
    pallas_call x0 -> x1, Pallas kernels: none -> 138 us  [fused_per_device(): pl.pallas_call(functools.partial(whole_kernel, (n_dp, n_t, chunks, rep, H...]
    all_gather x4 -> x0, waiting for transfers between devices: 136 us -> none  [the longest x1 50.3 us: per_device(): gathered = lax.all_gather(normed_input, 'tensor', axis=0, tiled=True)]
    reduce_scatter x2 -> x0, waiting for transfers between devices: 69.5 us -> none  [the longest x1 36.1 us: per_device(): lax.psum_scatter(lax.dot_general(block, joined, contract_first, preferred...]
    dot_general x13 -> x0, matrix products: 51.2 us -> none  [the longest x3 13.8 us: per_device(): jnp.dot(gathered, piece, preferred_element_type=jnp.float32)]
    psum x1 -> x0, blocking collectives: 40.3 us -> none  [per_device(): grad_pre = lax.psum(pre_part, ('dp', 'tensor'))]
    reduce_sum x4 -> x0, other arithmetic: 7.41 us -> none  [the longest x1 2.7 us: attend_backward(): value_heads.reshape(segment_length, heads // repeat, repeat, width).sum(2)]
    slice x4 -> x0, local copies, waits for them, and re-layouts: 4.78 us -> none  [the longest x1 2.3 us: per_device(): grad_query = grads[:, :width_query]]
    reshape x1 -> x6, local copies, waits for them, and re-layouts: 1.56 us -> 5.37 us  [the longest x1 1.31 us: fused_per_device(): cot = cotangent.reshape(block, chunks, qw).transpose(1, 0, 2)]
  transfers between devices with their start and end apart: 6 -> 0, of which waited for: 6 -> 0; matrix products, arithmetic and copies ran while one was open for 8% -> 0% of each run, Pallas kernels for 0% -> 0%
where the time goes in v1:
time: 155 us
  Pallas kernels  138 us (89%)
  local copies, waits for them, and re-layouts  12.2 us (8%)
  other arithmetic  3.66 us (2%)
    pallas_call x1, Pallas kernels, fused_per_device(): pl.pallas_call(functools.partial(whole_kernel, (n_dp, n_t, chunks, rep, H...  138 us
    unnamed x19, local copies, waits for them, and re-layouts  3.76 us

profile of v1, /device:TPU:0, one launch (start us, length us, event | category | flops | bytes accessed | tf_op | source)
XLA Modules:
  0.0 155.1 jit_solution(1893803255078558386)
XLA Ops:
  0.6 0.0 copy-start
  0.6 0.0 copy-start.3
  0.7 0.1 fusion.4
  0.8 0.1 pad_maximum_fusion
  0.9 0.6 tile.12
  1.5 0.6 tile.14
  2.2 0.0 copy-done
  2.2 1.1 copy_bitcast_fusion.3
  3.2 0.0 copy-done.3
  3.3 0.0 copy-start.1
  3.3 1.1 maximum_bitcast_fusion.own_ref
  4.4 0.5 copy-done.1
  5.0 0.5 copy.15
  5.5 0.0 copy-start.5
  5.5 1.3 copy.16
  6.8 0.1 fusion.1
  6.9 0.7 tile.31
  7.6 0.0 copy-done.5
  7.6 0.6 broadcast_in_dim.2.gain_ref
  8.2 138.5 %shard_map.109 = (bf16[4,512,256]{2,1,0:T(8,128)(2,1)}, bf16[128,2304]{1,0:T(8,128)(2,1)}, bf16[4,288,512]{2,1,0:T(8,128)(2,1)}, f32[1,2304]{1,0:T(1,128)}) custom-call(bf16[128,2304]{1,0:T(8,128)(2,1)} %tok_ref.1, f32[1,2304]{1,0:T(1,128)} %broadcast_in_dim.2.gain_ref, bf16[4,288,512]{2,1,0:T(8,128)(2,1)} %maximum_bitcast_fusion.own_ref, ...), custom_call_target="tpu_custom_call" | custom-call | tf_op jit(solution)/shard_map/pallas_call | solution.py:656
  146.7 1.6 %convert_element_type.11 = f32[4,288,512]{2,1,0:T(8,128)S(1)} convert(bf16[4,288,512]{2,1,0:T(8,128)(2,1)} %get-tuple-element.12) | non-fusion elementwise | flops 589824 | bytes 3538944 | tf_op jit(solution)/shard_map/convert_element_type | solution.py:697
  148.2 0.1 slice_bitcast_fusion.1
  148.3 0.9 copy.33
  149.2 0.9 copy.34
  150.1 0.1 slice_bitcast_fusion
  150.2 0.0 copy-start.2
  150.3 1.2 copy.25
  151.4 0.3 copy-done.2
  151.8 0.5 copy.17
  152.3 0.0 copy-start.6
  152.3 0.0 copy-start.4
  152.3 1.3 copy.21
  153.7 0.0 copy-done.6
  153.7 0.6 reduce
  154.3 0.0 copy-done.4
  154.3 0.8 copy.37
  (3 shorter events, 0.1 us)
Async XLA Ops:
  0.6 1.6 copy-start
  0.6 2.6 %copy-start.3 = (bf16[288,1024]{1,0:T(8,128)(2,1)S(1)}, bf16[288,1024]{1,0:T(8,128)(2,1)}, u32[]{:S(2)}) copy-start(bf16[288,1024]{1,0:T(8,128)(2,1)} %param.9) | copy-start | bytes 1769476
  3.3 1.7 %copy-start.1 = (bf16[512,1024]{1,0:T(8,128)(2,1)S(1)}, bf16[512,1024]{1,0:T(8,128)(2,1)}, u32[]{:S(2)}) copy-start(bf16[512,1024]{1,0:T(8,128)(2,1)} %param.7) | copy-start | bytes 3145732
  5.5 2.1 %copy-start.5 = (f32[2304]{0:T(1024)S(1)}, f32[2304]{0:T(1024)}, u32[]{:S(2)}) copy-start(f32[2304]{0:T(1024)} %param.8) | copy-start | bytes 27652
  150.2 1.5 copy-start.2
  152.3 1.3 copy-start.6
  152.3 2.0 %copy-start.4 = (bf16[128,2304]{1,0:T(8,128)(2,1)S(1)}, bf16[128,2304]{1,0:T(8,128)(2,1)}, u32[]{:S(2)}) copy-start(bf16[128,2304]{1,0:T(8,128)(2,1)} %get-tuple-element.36) | copy-start | bytes 1769476

commit v2 on v1

--- a/solution.py
+++ b/solution.py
@@ -2,6 +2,7 @@
 
 import jax
 import jax.numpy as jnp
+import numpy as np
 from jax import lax
 from jax.experimental import pallas as pl
 from jax.experimental.pallas import tpu as pltpu
@@ -195,14 +196,18 @@
     dims,
     tok_ref,
     gain_ref,
-    own_ref,
+    wq_ref,
+    wk_ref,
+    wv_ref,
     cot_ref,
     cos_ref,
     sin_ref,
     mask_ref,
     att_ref,
     gtok_ref,
-    grad_ref,
+    gq_ref,
+    gk_ref,
+    gv_ref,
     gpre_ref,
     x,
     xt,
@@ -228,17 +233,38 @@
     zr,
     ps,
     prs,
+    ls,
 ):
     n_dp, n_t, chunks, rep, hd = dims
     dp = lax.axis_index("dp")
     t = lax.axis_index("tensor")
     rows = tok_ref.shape[0]
     width = tok_ref.shape[1]
-    shard = own_ref.shape[1]
+    shard = wq_ref.shape[0]
+    qw = rep * hd
+    cw = qw + 2 * hd
     half = shard // 2
     core = lax.rem(dp, 2)
     chip = lax.div(dp, 2)
     mate, px, py = dp ^ 1, dp ^ 2, dp ^ 4
+
+    def own_copies(j):
+        here = pl.ds(pl.multiple_of(dp * shard, 16), shard)
+        return (
+            pltpu.make_async_copy(
+                wq_ref.at[:, j * qw : (j + 1) * qw], w.at[j, here, 0:qw], ls.at[0, j]
+            ),
+            pltpu.make_async_copy(
+                wk_ref.at[:, j * hd : (j + 1) * hd], w.at[j, here, qw : qw + hd], ls.at[1, j]
+            ),
+            pltpu.make_async_copy(
+                wv_ref.at[:, j * hd : (j + 1) * hd], w.at[j, here, qw + hd : cw], ls.at[2, j]
+            ),
+        )
+
+    for j in range(chunks):
+        for copy in own_copies(j):
+            copy.start()
 
     barrier = pltpu.get_barrier_semaphore()
     for o in range(1, n_dp):
@@ -266,18 +292,24 @@
             return pl.ds(pl.multiple_of(who * shard, 16), shard)
         return pl.ds(pl.multiple_of(who * shard + h * half, 16), half)
 
-    def wcopy(kind, j, origin, to, src=None, h=None):
+    def wcopy(kind, j, origin, to, h=None):
         place = w.at[j, wrow(origin, h)]
-        return rdma(place if src is None else src, place, ws.at[kind, j], wr.at[kind, j], to, t)
+        return rdma(place, place, ws.at[kind, j], wr.at[kind, j], to, t)
+
+    def offer(j):
+        wcopy(0, j, dp, px).start()
+        wcopy(1, j, dp, py).start()
 
     for j in range(chunks):
-        wcopy(0, j, dp, px, own_ref.at[j]).start()
-        wcopy(1, j, dp, py, own_ref.at[j]).start()
+        for copy in own_copies(j):
+            copy.wait()
+        if j < 2:
+            offer(j)
 
     tokens = tok_ref[...].astype(F32)
     inv = lax.rsqrt(jnp.mean(tokens * tokens, -1, keepdims=True) + EPS)
     x[pl.ds(pl.multiple_of(t * rows, rows), rows), :] = (
-        (tokens * inv) * gain_ref[...]
+        (tokens * inv) * gain_ref[...][None, :]
     ).astype(BF16)
 
     def xcopy(way, o, origin, to):
@@ -293,8 +325,7 @@
         xcopy(1, 0, t, t - 1).start()
 
     for j in range(chunks):
-        wcopy(2, j, dp, mate, own_ref.at[j]).start()
-        w[j, wrow(dp), :] = own_ref[j]
+        wcopy(2, j, dp, mate).start()
 
     def relay(j):
         wcopy(0, j, px, px).wait_recv()
@@ -326,33 +357,38 @@
         wcopy(6, j, dp ^ 6, px, h=1).wait_recv()
         wcopy(7, j, dp ^ 6, mate).start()
 
-    relay(0)
-    relay(1)
-    xrelay(1)
-    relay(2)
-    relay(3)
-    xrelay(2)
-    for j in range(chunks):
+    def ready(j):
         far(j)
-    xrelay(3)
-    for j in range(chunks):
         wcopy(2, j, mate, mate).wait_recv()
         wcopy(3, j, dp ^ 3, mate).wait_recv()
         wcopy(4, j, dp ^ 5, mate).wait_recv()
         wcopy(7, j, dp ^ 7, mate).wait_recv()
 
-    qw = rep * hd
-    cw = qw + 2 * hd
     factor = query_scalar ** (-0.5)
-    blocks = x.shape[0] // rows
-
-    xt[...] = x[...].T
-
-    def head(j, carry):
-        proj[...] = lax.dot_general(x[...], w[j], NN, preferred_element_type=F32)
-
-        def block(r, c2):
-            here = pl.ds(pl.multiple_of(r * rows, rows), rows)
+    low = t < n_t // 2
+    sign = jnp.where(low, 1, -1)
+    m = jnp.where(low, t, n_t - 1 - t)
+    fwd = jnp.where(low, 0, 1)
+
+    def mirror(b):
+        return jnp.where(low, b, n_t - 1 - b)
+
+    places = (
+        t,
+        jnp.where(m == 0, t + sign, t - sign),
+        jnp.where(m == 0, t + 2 * sign, t + sign),
+        mirror(n_t - 1),
+    )
+
+    def head_cols(j, i):
+        return pl.ds(pl.multiple_of(j * qw + i * hd, hd), hd)
+
+    def tiles(*which):
+        for slot, (j, p) in enumerate(which):
+            here = pl.ds(pl.multiple_of(places[p] * rows, rows), rows)
+            proj[slot] = lax.dot_general(x[here, :], w[j], NN, preferred_element_type=F32)
+        for slot, (j, p) in enumerate(which):
+            here = pl.ds(pl.multiple_of(places[p] * rows, rows), rows)
             cosv, sinv = cos_ref[...], sin_ref[...]
 
             def turn(v):
@@ -362,12 +398,12 @@
                 return v * cosv - swap_halves(v) * sinv
 
             q = jnp.concatenate(
-                [turn(proj[here, i * hd : (i + 1) * hd]).astype(BF16) for i in range(rep)], 0
+                [turn(proj[slot, :, i * hd : (i + 1) * hd]).astype(BF16) for i in range(rep)], 0
             )
-            k = turn(proj[here, qw : qw + hd]).astype(BF16)
-            v = proj[here, qw + hd : cw].astype(BF16)
+            k = turn(proj[slot, :, qw : qw + hd]).astype(BF16)
+            v = proj[slot, :, qw + hd : cw].astype(BF16)
             cot = jnp.concatenate(
-                [cot_ref[j, here, i * hd : (i + 1) * hd] for i in range(rep)], 0
+                [cot_ref[here, head_cols(j, i)] for i in range(rep)], 0
             )
             bent = jnp.tanh(
                 lax.dot_general(q, k, NT, preferred_element_type=F32) * factor / CAP
@@ -384,39 +420,25 @@
             dv = lax.dot_general(probs, cot, TN, preferred_element_type=F32)
             for i in range(rep):
                 part = slice(i * rows, (i + 1) * rows)
-                att_ref[j, here, i * hd : (i + 1) * hd] = att[part]
+                att_ref[here, head_cols(j, i)] = att[part]
                 dproj[j, here, i * hd : (i + 1) * hd] = unturn(dq[part]).astype(BF16)
             dproj[j, here, qw : qw + hd] = unturn(dk).astype(BF16)
             dproj[j, here, qw + hd : cw] = dv.astype(BF16)
-            return c2
-
-        lax.fori_loop(0, blocks, block, 0)
-        return carry
-
-    lax.fori_loop(0, chunks, head, 0)
-
-    low = t < n_t // 2
-    sign = jnp.where(low, 1, -1)
-    m = jnp.where(low, t, n_t - 1 - t)
-    fwd = jnp.where(low, 0, 1)
-
-    def mirror(b):
-        return jnp.where(low, b, n_t - 1 - b)
-
     def zcopy(way, b, to):
         src = dn.at[pl.ds(pl.multiple_of(b * rows, rows), rows)]
         return rdma(src, rb.at[way, b], zs.at[way, b], zr.at[way, b], dp, to)
 
     tile = 256
 
-    def back(i, carry):
-        b = mirror(n_t - 1 - i)
-        here = pl.ds(pl.multiple_of(b * rows, rows), rows)
+    def back(first, count):
+        here = pl.ds(pl.multiple_of(first * rows, rows), count * rows)
 
         def cols(n, c2):
             span = pl.ds(pl.multiple_of(n * tile, tile), tile)
-            total = jnp.zeros((rows, tile), F32)
-            for j in range(chunks):
+            total = lax.dot_general(
+                dproj[0, here, :], w[0, span, :], NT, preferred_element_type=F32
+            )
+            for j in range(1, chunks):
                 total += lax.dot_general(
                     dproj[j, here, :], w[j, span, :], NT, preferred_element_type=F32
                 )
@@ -425,13 +447,8 @@
 
         lax.fori_loop(0, width // tile, cols, 0)
 
-        @pl.when((m == 0) & (i < n_t - 1))
-        def _():
-            zcopy(fwd, b, t + sign).start()
-
-        return carry
-
-    lax.fori_loop(0, n_t, back, 0)
+    def outward(b):
+        zcopy(fwd, mirror(b), t + sign).start()
 
     def gcopy(kind, j, src, dst, to):
         return rdma(src, dst, gs.at[kind, j], gr.at[kind, j], to, t)
@@ -467,15 +484,16 @@
         return total.astype(BF16)
 
     def product(j):
-        for c in range(n_dp // 2):
+        def share(c, c2):
             for k in range(2):
-                who = 2 * c + k
+                span = pl.ds(pl.multiple_of((2 * c + k) * shard, 16), shard)
                 g[j, c, k] = lax.dot_general(
-                    xt[who * shard : (who + 1) * shard, :],
-                    dproj[j],
-                    NN,
-                    preferred_element_type=F32,
+                    xt[span, :], dproj[j], NN, preferred_element_type=F32
                 ).astype(BF16)
+            return c2
+
+        lax.fori_loop(0, n_dp // 2, share, 0)
+        to_mate(j).start()
 
     def on_chip(j):
         to_mate(j).wait_recv()
@@ -494,32 +512,63 @@
         cs[j, cx, hi] = add(cs[j, cx, hi], dr[j, hi])
         x_hi(j).start()
 
-    def grads_step(j, carry):
-        @pl.when(j < chunks)
-        def _():
-            product(j)
-            to_mate(j).start()
-
-        @pl.when(j > 0)
-        def _():
-            on_chip(j - 1)
-
-        return carry
-
-    lax.fori_loop(0, chunks + 1, grads_step, 0)
-
     def zsum(way, b):
         here = pl.ds(pl.multiple_of(b * rows, rows), rows)
         zcopy(way, b, t).wait_recv()
         dn[here, :] = add(dn[here, :], rb[way, b])
 
+    far_block = mirror(n_t - 1)
+    rest = jnp.where(low, 0, 1)
+
+    relay(0)
+    offer(2)
+    relay(1)
+    offer(3)
+    xrelay(1)
+    ready(0)
+    tiles((0, 0), (0, 1))
+    relay(2)
+    ready(1)
+    xrelay(2)
+    tiles((1, 0), (1, 1))
+    tiles((0, 2), (1, 2))
+    relay(3)
+    ready(2)
+    tiles((2, 0), (2, 1), (2, 2))
+    ready(3)
+    xrelay(3)
+    tiles((0, 3), (1, 3))
+    xt[...] = x[...].T
+    product(0)
+    tiles((2, 3), (3, 3))
+    back(far_block, 1)
+
+    @pl.when(m == 0)
+    def _():
+        outward(n_t - 1)
+
+    on_chip(0)
+    product(1)
+    tiles((3, 0), (3, 1), (3, 2))
+    back(rest, n_t - 1)
+
+    @pl.when(m == 0)
+    def _():
+        outward(n_t - 2)
+        outward(1)
+
+    on_chip(1)
+    product(2)
+
     @pl.when(m > 0)
     def _():
-        b = mirror(n_t - 1)
-        zsum(fwd, b)
-        zcopy(fwd, b, t + sign).start()
-
+        zsum(fwd, far_block)
+        outward(n_t - 1)
+
+    product(3)
+    on_chip(2)
     pass_on(0)
+    on_chip(3)
     pass_on(1)
 
     @pl.when(m > 0)
@@ -527,9 +576,8 @@
         b = mirror(0)
         zsum(1 - fwd, b)
         zcopy(1 - fwd, b, t - sign).start()
-        b2 = mirror(n_t - 2)
-        zsum(fwd, b2)
-        zcopy(fwd, b2, t + sign).start()
+        zsum(fwd, mirror(n_t - 2))
+        outward(n_t - 2)
 
     pass_on(2)
     pass_on(3)
@@ -565,7 +613,7 @@
 
     for o in range(1, n_dp):
         p1(o).start()
-    e = d_normed * gain_ref[...]
+    e = d_normed * gain_ref[...][None, :]
     gtok_ref[...] = (inv2 * (e - unit * jnp.mean(e * unit, -1, keepdims=True))).astype(BF16)
     for o in range(1, n_dp):
         p1r(o).wait_recv()
@@ -581,19 +629,22 @@
         y_hi(j).wait_recv()
         y_lo(j).wait_recv()
         x_hi(j).wait_recv()
-        grad_ref[j] = add(cs[j, chip], ar[0, j], ar[1, j])
+        done = add(cs[j, chip], ar[0, j], ar[1, j])
+        gq_ref[:, j * qw : (j + 1) * qw] = done[:, :qw]
+        gk_ref[:, j * hd : (j + 1) * hd] = done[:, qw : qw + hd]
+        gv_ref[:, j * hd : (j + 1) * hd] = done[:, qw + hd :]
 
     for o in range(1, n_t):
         p2r(o).wait_recv()
     total = pb2[0]
     for o in range(1, n_t):
         total = total + pb2[o]
-    gpre_ref[...] = total
+    gpre_ref[...] = total[0]
 
     for j in range(chunks):
-        wcopy(0, j, dp, px, own_ref.at[j]).wait_send()
-        wcopy(1, j, dp, py, own_ref.at[j]).wait_send()
-        wcopy(2, j, dp, mate, own_ref.at[j]).wait_send()
+        wcopy(0, j, dp, px).wait_send()
+        wcopy(1, j, dp, py).wait_send()
+        wcopy(2, j, dp, mate).wait_send()
         wcopy(3, j, px, mate).wait_send()
         wcopy(4, j, py, mate).wait_send()
         wcopy(5, j, px, py, h=0).wait_send()
@@ -635,39 +686,36 @@
     rep = w_query.shape[1] // key_weight.shape[1]
     qw = rep * HEAD_SIZE
     cw = qw + 2 * HEAD_SIZE
-    parts = (
-        w_query.reshape(shard, chunks, qw),
-        key_weight.reshape(shard, chunks, HEAD_SIZE),
-        value_weight.reshape(shard, chunks, HEAD_SIZE),
-    )
-    own = jnp.concatenate(parts, -1).transpose(1, 0, 2)
-    cot = cotangent.reshape(block, chunks, qw).transpose(1, 0, 2)
-    cosine, sine = rotary_tables(SEQ_LEN, HEAD_SIZE // 2)
-    reps = rows // SEQ_LEN
-    cosine = jnp.tile(jnp.concatenate([cosine[:, 0], cosine[:, 0]], -1), (reps, 1))
-    sine = jnp.tile(jnp.concatenate([-sine[:, 0], sine[:, 0]], -1), (reps, 1))
-    place = jnp.arange(rows)
+    half = HEAD_SIZE // 2
+    place = np.arange(rows)
+    freqs = BASE ** (-np.arange(half) / half)
+    angles = (place % SEQ_LEN)[:, None] * freqs[None, :]
+    cosine = np.concatenate([np.cos(angles)] * 2, -1).astype(np.float32)
+    sine = np.concatenate([-np.sin(angles), np.sin(angles)], -1).astype(np.float32)
     mask = (place[None, :] <= place[:, None]) & (
         place[None, :] // SEQ_LEN == place[:, None] // SEQ_LEN
     )
-    mask = jnp.tile(mask.astype(F32), (rep, 1))
+    mask = np.tile(mask.astype(np.float32), (rep, 1))
     vmem = pl.BlockSpec(memory_space=pltpu.VMEM)
+    hbm = pl.BlockSpec(memory_space=pl.ANY)
     dma = pltpu.SemaphoreType.DMA
-    att, grad_tokens, grads, grad_pre = pl.pallas_call(
+    attended, grad_tokens, gq, gk, gv, grad_pre = pl.pallas_call(
         functools.partial(whole_kernel, (n_dp, n_t, chunks, rep, HEAD_SIZE)),
         out_shape=(
-            jax.ShapeDtypeStruct((chunks, block, qw), BF16),
+            jax.ShapeDtypeStruct((block, chunks * qw), BF16),
             jax.ShapeDtypeStruct((rows, width), BF16),
-            jax.ShapeDtypeStruct((chunks, shard, cw), BF16),
-            jax.ShapeDtypeStruct((1, width), F32),
+            jax.ShapeDtypeStruct((shard, chunks * qw), BF16),
+            jax.ShapeDtypeStruct((shard, chunks * HEAD_SIZE), BF16),
+            jax.ShapeDtypeStruct((shard, chunks * HEAD_SIZE), BF16),
+            jax.ShapeDtypeStruct((width,), F32),
         ),
-        in_specs=[vmem] * 7,
-        out_specs=(vmem,) * 4,
+        in_specs=[vmem, vmem, hbm, hbm, hbm] + [vmem] * 4,
+        out_specs=(vmem,) * 6,
         scratch_shapes=[
             pltpu.VMEM((block, width), BF16),
             pltpu.VMEM((width, block), BF16),
             pltpu.VMEM((chunks, width, cw), BF16),
-            pltpu.VMEM((block, cw), F32),
+            pltpu.VMEM((3, rows, cw), F32),
             pltpu.VMEM((chunks, block, cw), BF16),
             pltpu.VMEM((chunks, n_dp // 2, 2, shard, cw), BF16),
             pltpu.VMEM((chunks, n_dp // 2, shard, cw), BF16),
@@ -688,23 +736,19 @@
             dma((2, n_t)),
             dma((2, n_dp)),
             dma((2, n_dp)),
+            dma((3, chunks)),
         ],
         compiler_params=pltpu.CompilerParams(
             collective_id=0, has_side_effects=True, vmem_limit_bytes=62 * 1024 * 1024
         ),
-    )(tokens, pre_gain[None, :], own, cot, cosine, sine, mask)
-    attended = att.transpose(1, 0, 2).reshape(block, chunks * qw)
-    grads = grads.astype(F32)
-    grad_query = grads[:, :, :qw].transpose(1, 0, 2).reshape(shard, chunks * qw)
-    grad_key = grads[:, :, qw : qw + HEAD_SIZE].transpose(1, 0, 2)
-    grad_value = grads[:, :, qw + HEAD_SIZE :].transpose(1, 0, 2)
+    )(tokens, pre_gain, w_query, key_weight, value_weight, cotangent, cosine, sine, mask)
     return (
         attended,
         grad_tokens,
-        grad_query,
-        grad_key.reshape(shard, chunks * HEAD_SIZE),
-        grad_value.reshape(shard, chunks * HEAD_SIZE),
-        grad_pre[0],
+        gq.astype(F32),
+        gk.astype(F32),
+        gv.astype(F32),
+        grad_pre,
     )
 
 

time: 155 us -> 121 us (0.78)
  Pallas kernels: 138 us -> 113 us
  local copies, waits for them, and re-layouts: 12.2 us -> 2.87 us
    pallas_call x1, Pallas kernels: 138 us -> 113 us  [fused_per_device(): pl.pallas_call(functools.partial(whole_kernel, (n_dp, n_t, chunks, rep, H...]
    reshape x6 -> x0, local copies, waits for them, and re-layouts: 5.37 us -> none  [the longest x1 1.31 us: fused_per_device(): cot = cotangent.reshape(block, chunks, qw).transpose(1, 0, 2)]
    convert_element_type x2 -> x3, other arithmetic: 1.67 us -> 4.04 us  [the longest x1 2.27 us: fused_per_device(): gq.astype(F32)]
    another operation x3 -> x0, local copies, waits for them, and re-layouts: 1.93 us -> none  [the longest x1 0.66 us: fused_per_device(): mask = jnp.tile(mask.astype(F32), (rep, 1))]
    unnamed x19 -> x13, local copies, waits for them, and re-layouts: 3.76 us -> 2.87 us
where the time goes in v2:
time: 121 us
  Pallas kernels  113 us (93%)
  other arithmetic  4.04 us (3%)
  local copies, waits for them, and re-layouts  2.87 us (2%)
    pallas_call x1, Pallas kernels, fused_per_device(): pl.pallas_call(functools.partial(whole_kernel, (n_dp, n_t, chunks, rep, H...  113 us
    unnamed x13, local copies, waits for them, and re-layouts  2.87 us

profile of v2, /device:TPU:0, one launch (start us, length us, event | category | flops | bytes accessed | tf_op | source)
XLA Modules:
  0.0 121.0 jit_solution(4241688360884376455)
XLA Ops:
  0.6 113.4 %shard_map.136 = (bf16[512,1024]{1,0:T(8,128)(2,1)}, bf16[128,2304]{1,0:T(8,128)(2,1)}, bf16[288,1024]{1,0:T(8,128)(2,1)}, bf16[288,512]{1,0:T(8,128)(2,1)}, bf16[288,512]{1,0:T(8,128)(2,1)}, /*index=5*/f32[2304]{0:T(1024)}) custom-call(bf16[128,2304]{1,0:T(8,128)(2,1)} %tok_ref.1, f32[2304]{0:T(1024)} %gain_ref.1, bf16[288,1024]{1,0:T(8,128)(2,1)} %wq_ref.1, ...), custom_call_target="tpu_custom_call" | custom-call | tf_op jit(solution)/shard_map/pallas_call | solution.py:702
  114.1 0.0 copy-start.3
  114.1 0.0 copy-start.2
  114.1 2.3 %convert_element_type.9 = f32[288,1024]{1,0:T(8,128)} convert(bf16[288,1024]{1,0:T(8,128)(2,1)} %get-tuple-element.14) | non-fusion elementwise | flops 294912 | bytes 1769472 | tf_op jit(solution)/shard_map/convert_element_type | solution.py:748
  116.4 0.0 copy-start
  116.4 0.0 copy-done.3
  116.4 0.9 convert_element_type.10
  117.2 0.0 copy-done.2
  117.3 0.9 convert_element_type.11
  118.1 0.0 copy-start.1
  118.1 0.0 copy-done
  118.1 0.0 copy-start.4
  118.1 1.0 copy.18
  119.1 0.5 copy-done.1
  119.6 0.8 copy.19
  120.4 0.0 copy-done.4
  120.4 0.6 copy.20
Async XLA Ops:
  114.1 2.3 %copy-start.3 = (bf16[288,512]{1,0:T(8,128)(2,1)S(1)}, bf16[288,512]{1,0:T(8,128)(2,1)}, u32[]{:S(2)}) copy-start(bf16[288,512]{1,0:T(8,128)(2,1)} %get-tuple-element.15) | copy-start | bytes 884740
  114.1 3.2 %copy-start.2 = (bf16[288,512]{1,0:T(8,128)(2,1)S(1)}, bf16[288,512]{1,0:T(8,128)(2,1)}, u32[]{:S(2)}) copy-start(bf16[288,512]{1,0:T(8,128)(2,1)} %get-tuple-element.16) | copy-start | bytes 884740
  116.4 1.8 %copy-start = (bf16[512,1024]{1,0:T(8,128)(2,1)S(1)}, bf16[512,1024]{1,0:T(8,128)(2,1)}, u32[]{:S(2)}) copy-start(bf16[512,1024]{1,0:T(8,128)(2,1)} %get-tuple-element.24) | copy-start | bytes 3145732
  118.1 1.4 %copy-start.1 = (bf16[128,2304]{1,0:T(8,128)(2,1)S(1)}, bf16[128,2304]{1,0:T(8,128)(2,1)}, u32[]{:S(2)}) copy-start(bf16[128,2304]{1,0:T(8,128)(2,1)} %get-tuple-element.25) | copy-start | bytes 1769476
  118.1 2.3 %copy-start.4 = (f32[2304]{0:T(1024)S(1)}, f32[2304]{0:T(1024)}, u32[]{:S(2)}) copy-start(f32[2304]{0:T(1024)} %get-tuple-element.29) | copy-start | bytes 27652

commit v3 on v2

--- a/solution.py
+++ b/solution.py
@@ -312,17 +312,21 @@
         (tokens * inv) * gain_ref[...][None, :]
     ).astype(BF16)
 
-    def xcopy(way, o, origin, to):
-        place = x.at[pl.ds(pl.multiple_of(origin * rows, rows), rows)]
-        return rdma(place, place, xs.at[way, o], xr.at[way, o], dp, to)
+    piece = rows // 2
+
+    def xcopy(way, o, h, origin, to):
+        place = x.at[pl.ds(pl.multiple_of(origin * rows + h * piece, piece), piece)]
+        return rdma(place, place, xs.at[way, o, h], xr.at[way, o, h], dp, to)
 
     @pl.when(t < n_t - 1)
     def _():
-        xcopy(0, 0, t, t + 1).start()
+        for h in range(2):
+            xcopy(0, 0, h, t, t + 1).start()
 
     @pl.when(t > 0)
     def _():
-        xcopy(1, 0, t, t - 1).start()
+        for h in range(2):
+            xcopy(1, 0, h, t, t - 1).start()
 
     for j in range(chunks):
         wcopy(2, j, dp, mate).start()
@@ -335,22 +339,22 @@
         wcopy(6, j, py, px, h=1).start()
         wcopy(4, j, py, mate).start()
 
-    def xrelay(o):
+    def xrelay(o, h):
         @pl.when(t - o >= 0)
         def _():
-            xcopy(0, o - 1, t - o, t).wait_recv()
+            xcopy(0, o - 1, h, t - o, t).wait_recv()
 
             @pl.when(t + 1 < n_t)
             def _():
-                xcopy(0, o, t - o, t + 1).start()
+                xcopy(0, o, h, t - o, t + 1).start()
 
         @pl.when(t + o < n_t)
         def _():
-            xcopy(1, o - 1, t + o, t).wait_recv()
+            xcopy(1, o - 1, h, t + o, t).wait_recv()
 
             @pl.when(t > 0)
             def _():
-                xcopy(1, o, t + o, t - 1).start()
+                xcopy(1, o, h, t + o, t - 1).start()
 
     def far(j):
         wcopy(5, j, dp ^ 6, py, h=0).wait_recv()
@@ -424,9 +428,16 @@
                 dproj[j, here, i * hd : (i + 1) * hd] = unturn(dq[part]).astype(BF16)
             dproj[j, here, qw : qw + hd] = unturn(dk).astype(BF16)
             dproj[j, here, qw + hd : cw] = dv.astype(BF16)
-    def zcopy(way, b, to):
-        src = dn.at[pl.ds(pl.multiple_of(b * rows, rows), rows)]
-        return rdma(src, rb.at[way, b], zs.at[way, b], zr.at[way, b], dp, to)
+    def zcopy(way, b, h, to):
+        src = dn.at[pl.ds(pl.multiple_of(b * rows + h * piece, piece), piece)]
+        return rdma(
+            src,
+            rb.at[way, b, pl.ds(h * piece, piece)],
+            zs.at[way, b, h],
+            zr.at[way, b, h],
+            dp,
+            to,
+        )
 
     tile = 256
 
@@ -447,8 +458,9 @@
 
         lax.fori_loop(0, width // tile, cols, 0)
 
-    def outward(b):
-        zcopy(fwd, mirror(b), t + sign).start()
+    def outward(b, halves=(0, 1)):
+        for h in halves:
+            zcopy(fwd, mirror(b), h, t + sign).start()
 
     def gcopy(kind, j, src, dst, to):
         return rdma(src, dst, gs.at[kind, j], gr.at[kind, j], to, t)
@@ -512,31 +524,34 @@
         cs[j, cx, hi] = add(cs[j, cx, hi], dr[j, hi])
         x_hi(j).start()
 
-    def zsum(way, b):
-        here = pl.ds(pl.multiple_of(b * rows, rows), rows)
-        zcopy(way, b, t).wait_recv()
-        dn[here, :] = add(dn[here, :], rb[way, b])
+    def zsum(way, b, h):
+        here = pl.ds(pl.multiple_of(b * rows + h * piece, piece), piece)
+        zcopy(way, b, h, t).wait_recv()
+        dn[here, :] = add(dn[here, :], rb[way, b, h * piece : (h + 1) * piece])
 
     far_block = mirror(n_t - 1)
     rest = jnp.where(low, 0, 1)
 
     relay(0)
     offer(2)
+    xrelay(1, 0)
     relay(1)
     offer(3)
-    xrelay(1)
+    xrelay(1, 1)
     ready(0)
     tiles((0, 0), (0, 1))
+    xrelay(2, 0)
     relay(2)
     ready(1)
-    xrelay(2)
+    xrelay(2, 1)
     tiles((1, 0), (1, 1))
     tiles((0, 2), (1, 2))
     relay(3)
     ready(2)
     tiles((2, 0), (2, 1), (2, 2))
     ready(3)
-    xrelay(3)
+    xrelay(3, 0)
+    xrelay(3, 1)
     tiles((0, 3), (1, 3))
     xt[...] = x[...].T
     product(0)
@@ -562,8 +577,9 @@
 
     @pl.when(m > 0)
     def _():
-        zsum(fwd, far_block)
-        outward(n_t - 1)
+        for h in range(2):
+            zsum(fwd, far_block, h)
+            outward(n_t - 1, (h,))
 
     product(3)
     on_chip(2)
@@ -574,20 +590,23 @@
     @pl.when(m > 0)
     def _():
         b = mirror(0)
-        zsum(1 - fwd, b)
-        zcopy(1 - fwd, b, t - sign).start()
-        zsum(fwd, mirror(n_t - 2))
-        outward(n_t - 2)
+        for h in range(2):
+            zsum(1 - fwd, b, h)
+            zcopy(1 - fwd, b, h, t - sign).start()
+            zsum(fwd, mirror(n_t - 2), h)
+            outward(n_t - 2, (h,))
 
     pass_on(2)
     pass_on(3)
 
     mine = pl.ds(pl.multiple_of(t * rows, rows), rows)
-    zcopy(1 - fwd, t, t).wait_recv()
+    for h in range(2):
+        zcopy(1 - fwd, t, h, t).wait_recv()
 
     @pl.when(m > 0)
     def _():
-        zcopy(fwd, t, t).wait_recv()
+        for h in range(2):
+            zcopy(fwd, t, h, t).wait_recv()
 
     @pl.when(m == 0)
     def _():
@@ -653,23 +672,24 @@
         to_mate(j).wait_send()
         for copy in (d_x, d_y, x_lo, x_hi, y_lo, y_hi):
             copy(j).wait_send()
-    for o in range(n_t - 1):
-        @pl.when((t - o >= 0) & (t + 1 < n_t))
+    for h in range(2):
+        for o in range(n_t - 1):
+            @pl.when((t - o >= 0) & (t + 1 < n_t))
+            def _():
+                xcopy(0, o, h, t - o, t + 1).wait_send()
+
+            @pl.when((t + o < n_t) & (t > 0))
+            def _():
+                xcopy(1, o, h, t + o, t - 1).wait_send()
+
+        for b in range(n_t - 1, 0, -1):
+            @pl.when(m < b)
+            def _():
+                zcopy(fwd, mirror(b), h, t + sign).wait_send()
+
+        @pl.when(m > 0)
         def _():
-            xcopy(0, o, t - o, t + 1).wait_send()
-
-        @pl.when((t + o < n_t) & (t > 0))
-        def _():
-            xcopy(1, o, t + o, t - 1).wait_send()
-
-    for b in range(n_t - 1, 0, -1):
-        @pl.when(m < b)
-        def _():
-            zcopy(fwd, mirror(b), t + sign).wait_send()
-
-    @pl.when(m > 0)
-    def _():
-        zcopy(1 - fwd, mirror(0), t - sign).wait_send()
+            zcopy(1 - fwd, mirror(0), h, t - sign).wait_send()
 
     for o in range(1, n_dp):
         p1(o).wait_send()
@@ -728,12 +748,12 @@
             pltpu.VMEM((n_t, 1, width), F32),
             dma((8, chunks)),
             dma((8, chunks)),
-            dma((2, n_t)),
-            dma((2, n_t)),
+            dma((2, n_t, 2)),
+            dma((2, n_t, 2)),
             dma((7, chunks)),
             dma((7, chunks)),
-            dma((2, n_t)),
-            dma((2, n_t)),
+            dma((2, n_t, 2)),
+            dma((2, n_t, 2)),
             dma((2, n_dp)),
             dma((2, n_dp)),
             dma((3, chunks)),

time: 121 us -> 118 us (0.975)
  Pallas kernels: 113 us -> 111 us
    pallas_call x1, Pallas kernels: 113 us -> 111 us  [fused_per_device(): pl.pallas_call(functools.partial(whole_kernel, (n_dp, n_t, chunks, rep, H...]
where the time goes in v3:
time: 118 us
  Pallas kernels  111 us (94%)
  other arithmetic  4.04 us (3%)
  local copies, waits for them, and re-layouts  2.87 us (2%)
    pallas_call x1, Pallas kernels, fused_per_device(): pl.pallas_call(functools.partial(whole_kernel, (n_dp, n_t, chunks, rep, H...  111 us
    unnamed x13, local copies, waits for them, and re-layouts  2.87 us

profile of v3, /device:TPU:0, one launch (start us, length us, event | category | flops | bytes accessed | tf_op | source)
XLA Modules:
  0.0 118.1 jit_solution(16745415017488691760)
XLA Ops:
  0.6 110.5 %shard_map.136 = (bf16[512,1024]{1,0:T(8,128)(2,1)}, bf16[128,2304]{1,0:T(8,128)(2,1)}, bf16[288,1024]{1,0:T(8,128)(2,1)}, bf16[288,512]{1,0:T(8,128)(2,1)}, bf16[288,512]{1,0:T(8,128)(2,1)}, /*index=5*/f32[2304]{0:T(1024)}) custom-call(bf16[128,2304]{1,0:T(8,128)(2,1)} %tok_ref.1, f32[2304]{0:T(1024)} %gain_ref.1, bf16[288,1024]{1,0:T(8,128)(2,1)} %wq_ref.1, ...), custom_call_target="tpu_custom_call" | custom-call | tf_op jit(solution)/shard_map/pallas_call | solution.py:722
  111.2 0.0 copy-start.3
  111.2 0.0 copy-start.2
  111.2 2.3 %convert_element_type.9 = f32[288,1024]{1,0:T(8,128)} convert(bf16[288,1024]{1,0:T(8,128)(2,1)} %get-tuple-element.14) | non-fusion elementwise | flops 294912 | bytes 1769472 | tf_op jit(solution)/shard_map/convert_element_type | solution.py:768
  113.5 0.0 copy-start
  113.5 0.0 copy-done.3
  113.5 0.9 convert_element_type.10
  114.4 0.0 copy-done.2
  114.4 0.9 convert_element_type.11
  115.3 0.0 copy-start.1
  115.3 0.0 copy-done
  115.3 0.0 copy-start.4
  115.3 1.0 copy.18
  116.2 0.5 copy-done.1
  116.7 0.8 copy.19
  117.5 0.0 copy-done.4
  117.5 0.6 copy.20
Async XLA Ops:
  111.2 2.3 %copy-start.3 = (bf16[288,512]{1,0:T(8,128)(2,1)S(1)}, bf16[288,512]{1,0:T(8,128)(2,1)}, u32[]{:S(2)}) copy-start(bf16[288,512]{1,0:T(8,128)(2,1)} %get-tuple-element.15) | copy-start | bytes 884740
  111.2 3.2 %copy-start.2 = (bf16[288,512]{1,0:T(8,128)(2,1)S(1)}, bf16[288,512]{1,0:T(8,128)(2,1)}, u32[]{:S(2)}) copy-start(bf16[288,512]{1,0:T(8,128)(2,1)} %get-tuple-element.16) | copy-start | bytes 884740
  113.5 1.8 %copy-start = (bf16[512,1024]{1,0:T(8,128)(2,1)S(1)}, bf16[512,1024]{1,0:T(8,128)(2,1)}, u32[]{:S(2)}) copy-start(bf16[512,1024]{1,0:T(8,128)(2,1)} %get-tuple-element.24) | copy-start | bytes 3145732
  115.3 1.4 %copy-start.1 = (bf16[128,2304]{1,0:T(8,128)(2,1)S(1)}, bf16[128,2304]{1,0:T(8,128)(2,1)}, u32[]{:S(2)}) copy-start(bf16[128,2304]{1,0:T(8,128)(2,1)} %get-tuple-element.25) | copy-start | bytes 1769476
  115.3 2.3 %copy-start.4 = (f32[2304]{0:T(1024)S(1)}, f32[2304]{0:T(1024)}, u32[]{:S(2)}) copy-start(f32[2304]{0:T(1024)} %get-tuple-element.29) | copy-start | bytes 27652
